TPU v7x, 32 devices: a whole 2x2x4 slice. The times are simulated.
32 devices in a mesh: aln: 4 (over y, x), rows: 8 (over z, core).
Axes of the slice: x: 2, y: 2, z: 4, core: 2. Of those that a mesh axis runs over, the one named last changes fastest.
Arguments:
- sequence_stack: bfloat16 [32, 8, 768], P(('aln', 'rows')), parts along dimension 0, may hold values from -6 to 6
- protein_spans: int32 [4], P('aln'), parts along dimension 0, may hold values from 1 to 8
- twofold_contacts: bfloat16 [32, 8, 128], P(('aln', 'rows')), parts along dimension 0, may hold values from -6 to 6
- horizontal_projection_triple: bfloat16 [768, 2304], P(None, 'rows'), may hold values from -0.21875 to 0.21875
- horizontal_projection_out: bfloat16 [768, 768], P(None, 'rows'), may hold values from -0.21875 to 0.21875
- vertical_projection_triple: bfloat16 [768, 2304], P(None, 'rows'), may hold values from -0.21875 to 0.21875
- vertical_projection_out: bfloat16 [768, 768], P(None, 'rows'), may hold values from -0.21875 to 0.21875
- contact_logit_offsets: bfloat16 [128, 12], replicated, may hold values from -0.5 to 0.5
- contact_projection_weights: bfloat16 [12, 128], replicated, may hold values from -1.75 to 1.75
Outputs:
- alignment_output: bfloat16 [32, 8, 768], P('aln', 'rows'), parts along dimension 0
- pair_feature_output: bfloat16 [32, 8, 128], P(('aln', 'rows')), parts along dimension 0
There are 4 independent parts, one for each index of `aln`. A program takes and returns all parts, laid end to end along the dimension named above; an argument that names none is the same for every part. Nothing has to cross between parts.
All inputs are finite; a program needn't handle non-finite values.
Results may differ from a plain program's by a relative error of at most 0.0075.
Values may be sent and summed in bfloat16 or wider, within the bound.
A program may use at most 64 MiB of HBM per device.

v0:
```python
import functools

import jax
import jax.numpy as jnp
from jax import lax
from jax.experimental import pallas as pl
from jax.experimental.pallas import tpu as pltpu
from jax.sharding import PartitionSpec as P


def normalize(incoming_sequence_stack):
    center = jnp.mean(incoming_sequence_stack, axis=-1, keepdims=True)
    spread = jnp.mean(jnp.square(incoming_sequence_stack - center), axis=-1, keepdims=True)
    return (incoming_sequence_stack - center) * lax.rsqrt(spread + 1e-05)


def split_three(packed, hidden_channel_size, head_count, shape_rows, shape_res):
    head_dim = hidden_channel_size // head_count
    queries = (packed[:, :hidden_channel_size] * head_dim ** (-0.5)).astype(jnp.bfloat16)
    key_rows = packed[:, hidden_channel_size : 2 * hidden_channel_size].astype(jnp.bfloat16)
    value_rows = packed[:, 2 * hidden_channel_size :].astype(jnp.bfloat16)
    input_dimensions = (shape_rows, shape_res, head_count, head_dim)
    return (
        queries.reshape(input_dimensions),
        key_rows.reshape(input_dimensions),
        value_rows.reshape(input_dimensions),
    )


def masked_softmax(scores, protein_spans):
    key_valid = lax.broadcasted_iota(jnp.int32, (1, 1, scores.shape[2]), 2) < protein_spans[0]
    return jax.nn.softmax(jnp.where(key_valid, scores, -1e30), axis=-1).astype(jnp.bfloat16)


def per_device(
    sequence_stack,
    protein_spans,
    twofold_contacts,
    horizontal_projection_triple,
    horizontal_projection_out,
    vertical_projection_triple,
    vertical_projection_out,
    contact_logit_offsets,
    contact_projection_weights,
):
    sequences_per_shard, sequence_positions, hidden_channel_size = sequence_stack.shape
    parties = lax.axis_size("rows")
    overall_sequence_number = sequences_per_shard * parties
    residue_portion = sequence_positions // parties
    head_count = contact_logit_offsets.shape[1]
    channels = contact_logit_offsets.shape[0]
    scale_rows = float(overall_sequence_number) ** (-0.5)
    incoming_sequence_stack = sequence_stack.astype(jnp.float32)
    normed = (
        normalize(incoming_sequence_stack).astype(jnp.bfloat16).reshape(-1, hidden_channel_size)
    )
    row_whole = lax.all_gather(horizontal_projection_triple, "rows", axis=1, tiled=True)
    packed = jnp.dot(normed, row_whole, preferred_element_type=jnp.float32)
    queries, key_rows, value_rows = split_three(
        packed, hidden_channel_size, head_count, sequences_per_shard, sequence_positions
    )
    partial_value = jnp.einsum(
        "rihe,rjhe->hij", queries, key_rows, preferred_element_type=jnp.float32
    )
    bias_own = jnp.dot(
        twofold_contacts.reshape(-1, channels),
        contact_logit_offsets,
        preferred_element_type=jnp.float32,
    )
    bias_own = bias_own.reshape(residue_portion, sequence_positions, head_count).transpose(2, 0, 1)
    owned = lax.psum_scatter(partial_value, "rows", scatter_dimension=1, tiled=True)
    scores = owned * scale_rows + bias_own
    probs_own = masked_softmax(scores, protein_spans)
    row_probs = lax.all_gather(probs_own, "rows", axis=1, tiled=True)
    flat_scores = scores.astype(jnp.bfloat16).transpose(1, 2, 0).reshape(-1, head_count)
    pair_feature_output = (
        twofold_contacts.astype(jnp.float32)
        + jnp.dot(
            flat_scores, contact_projection_weights, preferred_element_type=jnp.float32
        ).reshape(residue_portion, sequence_positions, channels)
    ).astype(jnp.bfloat16)
    blended = jnp.einsum(
        "hij,rjhe->rihe", row_probs, value_rows, preferred_element_type=jnp.float32
    )
    blended = blended.astype(jnp.bfloat16).reshape(-1, hidden_channel_size)
    out_whole = lax.all_gather(horizontal_projection_out, "rows", axis=1, tiled=True)
    attended = jnp.dot(blended, out_whole, preferred_element_type=jnp.float32)
    updated_alignment = (
        incoming_sequence_stack
        + attended.reshape(sequences_per_shard, sequence_positions, hidden_channel_size)
    ).astype(jnp.bfloat16)
    columns = lax.all_to_all(updated_alignment, "rows", split_axis=1, concat_axis=0, tiled=True)
    column_input_rows = columns.astype(jnp.float32)
    col_normed = normalize(column_input_rows).astype(jnp.bfloat16).reshape(-1, hidden_channel_size)
    col_whole = lax.all_gather(vertical_projection_triple, "rows", axis=1, tiled=True)
    col_packed = jnp.dot(col_normed, col_whole, preferred_element_type=jnp.float32)
    col_queries, col_keys, col_values = split_three(
        col_packed, hidden_channel_size, head_count, overall_sequence_number, residue_portion
    )
    logits = jnp.einsum(
        "alhe,blhe->lhab", col_queries, col_keys, preferred_element_type=jnp.float32
    )
    col_probs = jax.nn.softmax(logits, axis=-1).astype(jnp.bfloat16)
    column_mixed_output = jnp.einsum(
        "lhab,blhe->alhe", col_probs, col_values, preferred_element_type=jnp.float32
    )
    column_mixed_output = column_mixed_output.astype(jnp.bfloat16).reshape(-1, hidden_channel_size)
    col_out_whole = lax.all_gather(vertical_projection_out, "rows", axis=1, tiled=True)
    column_attention_result = jnp.dot(
        column_mixed_output, col_out_whole, preferred_element_type=jnp.float32
    )
    alignment_output = (
        column_input_rows
        + column_attention_result.reshape(
            overall_sequence_number, residue_portion, hidden_channel_size
        )
    ).astype(jnp.bfloat16)
    return (alignment_output, pair_feature_output)


LANES = 128
BF = jnp.bfloat16
F32 = jnp.float32


def iota(shape, axis):
    return lax.broadcasted_iota(jnp.int32, shape, axis)


def dot(a, b, ca=1, cb=0, precision=None):
    return lax.dot_general(
        a, b, (((ca,), (cb,)), ((), ())), preferred_element_type=F32, precision=precision
    )


def exchange_partner(me, k, n):
    at, bit = me, 1
    while bit < n:
        if k & bit:
            at = at + bit * (1 - 2 * lax.rem(me // bit, 2))
        bit *= 2
    return at


def gathered_tile(slabs, width, tile):
    total = None
    for d in range(slabs.shape[0]):
        first = (width * d) // LANES
        last = (width * (d + 1) - 1) // LANES
        if first <= tile <= last:
            at = (tile - first) * LANES
            piece = slabs[d, :, at : at + LANES]
            total = piece if total is None else total + piece
    return total


def fused_kernel(
    n,
    copies,
    cuts,
    head_dim,
    seq_hbm,
    span_ref,
    con_hbm,
    offs_ref,
    cw_ref,
    w1_hbm,
    o1_hbm,
    w2_hbm,
    o2_hbm,
    out_ref,
    pair_ref,
    w1,
    o1,
    w2,
    seq_all,
    pk1,
    up_all,
    pk2,
    got,
    o2_all,
    load_sem,
    send_sem,
    recv_sem,
):
    me = lax.axis_index("rows")
    peers = [exchange_partner(me, k, n) for k in range(n)]
    order = list(range(n - 1, 0, -1))
    mine_a = lax.axis_index("aln")
    twins = [exchange_partner(mine_a, q, copies) for q in range(copies)]
    far_first = [k for k in order if k % 2 == 0]
    near_first = far_first[::-1]
    other = peers[1]
    length, width_d = seq_hbm.shape
    heads, channels = offs_ref.shape
    w_cols = w1_hbm.shape[0]
    o_cols = o1_hbm.shape[0]
    shift = pl.multiple_of(lax.rem(w_cols * me, LANES), 16)

    loads = [
        pltpu.make_async_copy(src, dst, load_sem.at[s])
        for s, (src, dst) in enumerate((
            (w1_hbm, w1.at[pl.ds(shift, w_cols)]),
            (o1_hbm, o1),
            (w2_hbm, w2.at[pl.ds(shift, w_cols)]),
            (o2_hbm, o2_all.at[me]),
            (seq_hbm, seq_all.at[me, :, pl.ds(0, width_d)]),
            (con_hbm, seq_all.at[me, :, pl.ds(width_d, channels)]),
        ))
    ]
    loads[4].start()
    loads[5].start()
    barrier = pltpu.get_barrier_semaphore()
    for k in order:
        pl.semaphore_signal(
            barrier, inc=1, device_id={"rows": peers[k]}, device_id_type=pl.DeviceIdType.MESH
        )
    for q in range(1, copies):
        pl.semaphore_signal(
            barrier,
            inc=1,
            device_id={"aln": twins[q], "rows": me},
            device_id_type=pl.DeviceIdType.MESH,
        )
    w1[...] = jnp.zeros_like(w1)
    w2[...] = jnp.zeros_like(w2)
    for c in loads[:4]:
        c.start()
    loads[4].wait()
    loads[5].wait()
    pl.semaphore_wait(barrier, n - 1 + copies - 1)

    sent = []

    def send(phase, k, src, dst, to=None, twin=0):
        c = pltpu.make_async_remote_copy(
            src_ref=src,
            dst_ref=dst,
            send_sem=send_sem.at[phase, k],
            recv_sem=recv_sem.at[phase, k],
            device_id={"aln": twins[twin], "rows": peers[k] if to is None else to},
            device_id_type=pl.DeviceIdType.MESH,
        )
        c.start()
        sent.append(c)

    def receive(phase, k, dst):
        pltpu.make_async_remote_copy(
            src_ref=dst,
            dst_ref=dst,
            send_sem=send_sem.at[phase, k],
            recv_sem=recv_sem.at[phase, k],
            device_id={"rows": peers[k]},
            device_id_type=pl.DeviceIdType.MESH,
        ).wait_recv()

    rows_c = o_cols // cuts[0]
    lanes_c = o2_hbm.shape[1] // cuts[1]

    def cut(slab, share):
        top = pl.multiple_of(share // cuts[1] * rows_c, rows_c)
        left = pl.multiple_of(lax.rem(share, cuts[1]) * lanes_c, lanes_c)
        return o2_all.at[slab, pl.ds(top, rows_c), pl.ds(left, lanes_c)]

    def spread(phase, slabs):
        for k in far_first:
            send(phase, k, slabs.at[me], slabs.at[me])
        send(phase, 1, slabs.at[me], slabs.at[me])

    def relay(phase, slabs):
        for k in near_first:
            receive(phase, k, slabs.at[peers[k]])
            send(phase, k + 1, slabs.at[peers[k]], slabs.at[peers[k]], other)

    def land(phase, slabs):
        receive(phase, 1, slabs.at[other])
        for k in near_first:
            receive(phase, k + 1, slabs.at[peers[k + 1]])

    def collect(phase, slabs):
        relay(phase, slabs)
        land(phase, slabs)

    for k in order:
        send(0, k, seq_all.at[me], seq_all.at[me])
    loads[3].wait()
    share = cut(me, mine_a)
    for k in far_first:
        send(5, k, share, share)
    send(5 + copies, 1, o2_all.at[me], o2_all.at[me])

    tokens = n * length
    per_tile = LANES // head_dim
    tiles = width_d // LANES
    hi = heads * length

    tok_r = iota((tokens, tokens), 0) // length
    tok_i = iota((tokens, tokens), 0) % length
    lane_r = iota((tokens, tokens), 1) // length
    lane_i = iota((tokens, tokens), 1) % length
    same_r = tok_r == lane_r
    same_i = tok_i == lane_i
    fold = jnp.where(same_i, 1.0, 0.0).astype(F32)
    lane = iota((tokens, LANES), 1)

    def split_heads(tile):
        f = tile.astype(F32)
        return jnp.concatenate(
            [
                jnp.where((lane >= s * head_dim) & (lane < (s + 1) * head_dim), f, 0.0)
                for s in range(per_tile)
            ],
            axis=0,
        ).astype(BF)

    def join_heads(stack):
        total = stack[:tokens]
        for s in range(1, per_tile):
            total = jnp.where(lane >= s * head_dim, stack[s * tokens : (s + 1) * tokens], total)
        return total

    def project(x, w, slot):
        slot[me] = dot(x, w[...], 1, 1).astype(BF)

    rows_f = [None] * n
    pick = jnp.where(iota((hi, heads), 0) // length == iota((hi, heads), 1), 1.0, 0.0)
    offs_rep = dot(pick.astype(BF), offs_ref[...]).astype(BF)
    mine = jnp.where(iota((hi, heads), 0) % length == me, pick, 0.0).astype(BF)
    cw_rep = dot(mine, cw_ref[...]).astype(BF)
    columns = iota((o_cols, width_d), 1) == iota((o_cols, width_d), 0) + o_cols * me
    columns = jnp.where(columns, 1.0, 0.0).astype(BF)

    for k in order:
        receive(0, k, seq_all.at[peers[k]])
    x = seq_all[:, :, :width_d].astype(F32).reshape(tokens, width_d)
    x_own = dot(x.astype(BF), columns, 1, 1)
    normed = normalize(x).astype(BF)
    loads[0].wait()
    project(normed, w1, pk1)
    spread(2, pk1)
    for k in near_first:
        share = cut(peers[k], mine_a)
        receive(5, k, share)
        for q in range(1, copies):
            send(5 + q, k, share, share, me, q)
    con = seq_all[:, :, width_d:].astype(F32).reshape(tokens, channels).astype(BF)
    bias = dot(offs_rep, con, 1, 1)
    own = iota((hi, tokens), 0) % length == iota((hi, tokens), 1) // length
    bias = jnp.where(own, bias, 0.0)
    collect(2, pk1)
    tied = []
    for t in range(tiles):
        q = split_heads(gathered_tile(pk1, w_cols, t))
        kk = gathered_tile(pk1, w_cols, tiles + t)
        s = dot(q, kk, 1, 1).reshape(per_tile, tokens, tokens)
        s = jnp.where(same_r[None], s, 0.0).reshape(per_tile, n, length, tokens)
        tied.append(jnp.sum(s, axis=1).reshape(per_tile * length, tokens))
    tied = jnp.concatenate(tied, axis=0)
    scale = head_dim ** (-0.5) * float(n) ** (-0.5)
    scores = dot(tied * scale + bias, fold, precision=lax.Precision.HIGHEST)

    key_ok = iota((hi, tokens), 1) % length < span_ref[0]
    logits = jnp.where(key_ok, scores, -1e30)
    e = jnp.exp(logits - jnp.max(logits, axis=1, keepdims=True))
    probs = e / (jnp.sum(e, axis=1, keepdims=True) * (1.0 / n))
    probs = probs.astype(BF).astype(F32)
    blended = []
    for t in range(tiles):
        rows = per_tile * length
        p = probs[t * rows : (t + 1) * rows].reshape(per_tile, 1, length, tokens)
        p = jnp.broadcast_to(p, (per_tile, n, length, tokens)).reshape(per_tile, tokens, tokens)
        p = jnp.where(same_r[None], p, 0.0).reshape(per_tile * tokens, tokens).astype(BF)
        v = gathered_tile(pk1, w_cols, 2 * tiles + t)
        blended.append(join_heads(dot(p, v)).astype(BF))
    blended = jnp.concatenate(blended, axis=1)
    loads[1].wait()
    up_all[me, :, :o_cols] = (x_own + dot(blended, o1[...], 1, 1)).astype(BF)
    spread(3, up_all)
    for k in near_first:
        for q in range(1, copies):
            receive(5 + q, k, cut(peers[k], twins[q]))
        send(5 + copies, k + 1, o2_all.at[peers[k]], o2_all.at[peers[k]], other)

    add = dot(scores.astype(BF), cw_rep, 0, 0)[:length]
    pair_ref[...] = (seq_all[me, :, width_d:].astype(F32) + add).astype(BF)

    collect(3, up_all)
    updated = jnp.concatenate(
        [up_all[d].astype(F32)[:, :o_cols] for d in range(n)], axis=1
    )
    perm = jnp.where((tok_r == lane_i) & (tok_i == lane_r), 1.0, 0.0).astype(BF)
    normed = dot(perm, normalize(updated).astype(BF)).astype(BF)
    loads[2].wait()
    pk2[...] = dot(normed, w2[...], 1, 1).reshape(length, n, w2.shape[0]).astype(BF)
    for k in order:
        send(4, k, pk2.at[peers[k]], got.at[me])
    got[me] = pk2[me]
    sel = (iota((n, tokens), 0) == iota((n, tokens), 1) // length) & (
        iota((n, tokens), 1) % length == me
    )
    residual = dot(jnp.where(sel, 1.0, 0.0).astype(BF), updated.astype(BF))
    for k in order:
        receive(4, k, got.at[peers[k]])
    lane_n = iota((n, LANES), 1)
    mixed = []
    for t in range(tiles):
        qf = gathered_tile(got, w_cols, t).astype(F32)
        q = jnp.concatenate(
            [
                jnp.where((lane_n >= h * head_dim) & (lane_n < (h + 1) * head_dim), qf, 0.0)
                for h in range(per_tile)
            ],
            axis=0,
        ).astype(BF)
        kk = gathered_tile(got, w_cols, tiles + t)
        s = dot(q, kk, 1, 1) * head_dim ** (-0.5)
        e = jnp.exp(s - jnp.max(s, axis=1, keepdims=True))
        p = (e / jnp.sum(e, axis=1, keepdims=True)).astype(BF)
        both = dot(p, gathered_tile(got, w_cols, 2 * tiles + t))
        total = both[:n]
        for h in range(1, per_tile):
            total = jnp.where(lane_n >= h * head_dim, both[h * n : (h + 1) * n], total)
        mixed.append(total)
    mixed = jnp.concatenate(mixed, axis=1).astype(BF)
    land(5 + copies, o2_all)
    final = jnp.concatenate(
        [dot(mixed, o2_all[d], 1, 1) for d in range(n)], axis=1
    )
    out_ref[...] = (residual + final).astype(BF)
    for c in sent:
        c.wait_send()


def fused_device(n, copies, cuts, seq, spans, con, w1, o1, w2, o2, offs, cw):
    _, length, width = seq.shape
    channels, heads = offs.shape
    w1, o1, w2, o2, offs = w1.T, o1.T, w2.T, o2.T, offs.T
    tokens = n * length
    window = max(
        -(-((w1.shape[0] * d) % LANES + w1.shape[0]) // LANES) for d in range(n)
    ) * LANES
    o_window = -(-o1.shape[0] // LANES) * LANES
    vmem = pl.BlockSpec(memory_space=pltpu.VMEM)
    hbm = pl.BlockSpec(memory_space=pl.ANY)
    out, pair = pl.pallas_call(
        functools.partial(fused_kernel, n, copies, cuts, width // heads),
        out_shape=(
            jax.ShapeDtypeStruct((n, width), BF),
            jax.ShapeDtypeStruct((length, channels), BF),
        ),
        in_specs=[hbm, pl.BlockSpec(memory_space=pltpu.SMEM), hbm, vmem, vmem, hbm, hbm, hbm, hbm],
        out_specs=(vmem, vmem),
        scratch_shapes=[
            pltpu.VMEM((window, width), BF),
            pltpu.VMEM(o1.shape, BF),
            pltpu.VMEM((window, width), BF),
            pltpu.VMEM((n, length, width + channels), BF),
            pltpu.VMEM((n, tokens, window), BF),
            pltpu.VMEM((n, tokens, o_window), BF),
            pltpu.VMEM((length, n, window), BF),
            pltpu.VMEM((n, n, window), BF),
            pltpu.VMEM((n, *o2.shape), BF),
            pltpu.SemaphoreType.DMA((6,)),
            pltpu.SemaphoreType.DMA((6 + copies, n)),
            pltpu.SemaphoreType.DMA((6 + copies, n)),
        ],
        compiler_params=pltpu.CompilerParams(collective_id=0, has_side_effects=True),
    )(seq.reshape(length, width), spans, con.reshape(length, channels), offs, cw, w1, o1, w2, o2)
    return out.reshape(n, 1, width), pair.reshape(1, length, channels)


def dispatch(n, copies, *args):
    seq, _, con, w1, o1 = args[:5]
    heads = args[7].shape[1]
    rows, length, width = seq.shape
    head_dim = width // heads
    fits = (
        rows == 1
        and con.shape[0] == 1
        and length == n
        and n % 8 == 0
        and n & (n - 1) == 0
        and w1.shape[1] % 16 == 0
        and n * length <= 256
        and width % LANES == 0
        and LANES % head_dim == 0
    )
    cuts = [
        (down, copies // down)
        for down in range(1, copies + 1)
        if copies % down == 0
        and args[4].shape[1] % (16 * down) == 0
        and width % (LANES * (copies // down)) == 0
    ]
    if fits and copies & (copies - 1) == 0 and cuts:
        return fused_device(n, copies, cuts[-1], *args)
    return per_device(*args)


def solution(mesh):
    placed = (
        P(("aln", "rows"), None, None),
        P("aln"),
        P(("aln", "rows"), None, None),
        P(None, "rows"),
        P(None, "rows"),
        P(None, "rows"),
        P(None, "rows"),
        P(),
        P(),
    )
    return jax.shard_map(
        functools.partial(dispatch, mesh.shape["rows"], mesh.shape["aln"]),
        mesh=mesh,
        in_specs=placed,
        out_specs=(P("aln", "rows", None), P(("aln", "rows"), None, None)),
        check_vma=False,
    )
```

profile of v0, /device:TPU:0, one launch (start us, length us, event | category | flops | bytes accessed | tf_op | source)
XLA Modules:
  0.0 34.5 jit_solution(11418851169639777996)
XLA Ops:
  1.3 31.3 %shard_map.104 = (bf16[8,768]{1,0:T(8,128)(2,1)}, bf16[8,128]{1,0:T(8,128)(2,1)}) custom-call(bf16[8,768]{1,0:T(8,128)(2,1)} %bitcast.13, s32[1]{0:T(128)S(6)} %copy.13.span_ref, bf16[8,128]{1,0:T(8,128)(2,1)} %bitcast.16, bf16[12,128]{1,0:T(8,128)(2,1)} %bitcast.15, bf16[12,128]{1,0:T(8,128)(2,1)} %cw_ref.1, bf16[288,768]{1,0:T(8,128)(2,1)} %bitcast.9, ...), custom_call_target="tpu_custom_call" | custom-call | tf_op jit(solution)/shard_map/pallas_call | solution.py:445
  32.6 0.0 copy-start
  32.6 1.3 %copy.14 = bf16[8,1,768]{2,0,1:T(8,128)(2,1)} copy(bf16[8,1,768]{2,0,1:T(8,128)(2,1)} %bitcast.14) | data formatting | bytes 24576
  33.9 0.0 copy-done
  33.9 0.6 %copy.15 = bf16[1,8,128]{2,1,0:T(8,128)(2,1)} copy(bf16[1,8,128]{2,1,0:T(8,128)(2,1)S(1)} %bitcast.17) | data formatting | bytes 4096
Async XLA Ops:
  32.6 1.3 %copy-start = (bf16[8,128]{1,0:T(8,128)(2,1)S(1)}, bf16[8,128]{1,0:T(8,128)(2,1)}, u32[]{:S(2)}) copy-start(bf16[8,128]{1,0:T(8,128)(2,1)} %get-tuple-element.5) | copy-start | bytes 6148
where the time goes:
time: 34.8 us; the launch traced here: 34.5 us
  Pallas kernels  31.3 us (90%)
  local copies, waits for them, and re-layouts  1.89 us (5%)
  between operations  1.29 us (4%)
    pallas_call x1, Pallas kernels, fused_device(): pl.pallas_call(functools.partial(fused_kernel, n, copies, cuts, width //...  31.3 us
    unnamed x4, local copies, waits for them, and re-layouts  1.89 us

commit v1 on v0

--- a/solution.py
+++ b/solution.py
@@ -162,8 +162,8 @@
     seq_hbm,
     span_ref,
     con_hbm,
-    offs_ref,
-    cw_ref,
+    offs_hbm,
+    cw_hbm,
     w1_hbm,
     o1_hbm,
     w2_hbm,
@@ -179,6 +179,8 @@
     pk2,
     got,
     o2_all,
+    offs_ref,
+    cw_ref,
     load_sem,
     send_sem,
     recv_sem,
@@ -206,10 +208,10 @@
             (o2_hbm, o2_all.at[me]),
             (seq_hbm, seq_all.at[me, :, pl.ds(0, width_d)]),
             (con_hbm, seq_all.at[me, :, pl.ds(width_d, channels)]),
+            (offs_hbm, offs_ref),
+            (cw_hbm, cw_ref),
         ))
     ]
-    loads[4].start()
-    loads[5].start()
     barrier = pltpu.get_barrier_semaphore()
     for k in order:
         pl.semaphore_signal(
@@ -222,37 +224,49 @@
             device_id={"aln": twins[q], "rows": me},
             device_id_type=pl.DeviceIdType.MESH,
         )
+    loads[4].start()
+    loads[5].start()
     w1[...] = jnp.zeros_like(w1)
     w2[...] = jnp.zeros_like(w2)
-    for c in loads[:4]:
+    for c in loads[:4] + loads[6:]:
         c.start()
     loads[4].wait()
     loads[5].wait()
     pl.semaphore_wait(barrier, n - 1 + copies - 1)
 
-    sent = []
-
-    def send(phase, k, src, dst, to=None, twin=0):
-        c = pltpu.make_async_remote_copy(
+    def send(phase, sem, k, src, dst, to=None, twin=0):
+        pltpu.make_async_remote_copy(
             src_ref=src,
             dst_ref=dst,
-            send_sem=send_sem.at[phase, k],
-            recv_sem=recv_sem.at[phase, k],
+            send_sem=send_sem.at[phase],
+            recv_sem=recv_sem.at[sem],
             device_id={"aln": twins[twin], "rows": peers[k] if to is None else to},
             device_id_type=pl.DeviceIdType.MESH,
-        )
-        c.start()
-        sent.append(c)
-
-    def receive(phase, k, dst):
+        ).start()
+
+    def finish(phase, ref):
         pltpu.make_async_remote_copy(
-            src_ref=dst,
-            dst_ref=dst,
-            send_sem=send_sem.at[phase, k],
-            recv_sem=recv_sem.at[phase, k],
-            device_id={"rows": peers[k]},
+            src_ref=ref,
+            dst_ref=ref,
+            send_sem=send_sem.at[phase],
+            recv_sem=recv_sem.at[0],
+            device_id={"rows": other},
+            device_id_type=pl.DeviceIdType.MESH,
+        ).wait_send()
+
+    def receive(sem, ref):
+        pltpu.make_async_remote_copy(
+            src_ref=ref,
+            dst_ref=ref,
+            send_sem=send_sem.at[0],
+            recv_sem=recv_sem.at[sem],
+            device_id={"rows": other},
             device_id_type=pl.DeviceIdType.MESH,
         ).wait_recv()
+
+    half = n // 2
+    AT_X, AT_A2A = 0, 1
+    AT_PK, AT_UP, AT_CUT, AT_TWIN = (2 + half * q for q in range(4))
 
     rows_c = o_cols // cuts[0]
     lanes_c = o2_hbm.shape[1] // cuts[1]
@@ -262,32 +276,24 @@
         left = pl.multiple_of(lax.rem(share, cuts[1]) * lanes_c, lanes_c)
         return o2_all.at[slab, pl.ds(top, rows_c), pl.ds(left, lanes_c)]
 
-    def spread(phase, slabs):
+    def spread(phase, at, slabs):
         for k in far_first:
-            send(phase, k, slabs.at[me], slabs.at[me])
-        send(phase, 1, slabs.at[me], slabs.at[me])
-
-    def relay(phase, slabs):
+            send(phase, at + k // 2, k, slabs.at[me], slabs.at[me])
+        send(phase, at, 1, slabs.at[me], slabs.at[me])
+
+    def collect(phase, at, slabs):
         for k in near_first:
-            receive(phase, k, slabs.at[peers[k]])
-            send(phase, k + 1, slabs.at[peers[k]], slabs.at[peers[k]], other)
-
-    def land(phase, slabs):
-        receive(phase, 1, slabs.at[other])
-        for k in near_first:
-            receive(phase, k + 1, slabs.at[peers[k + 1]])
-
-    def collect(phase, slabs):
-        relay(phase, slabs)
-        land(phase, slabs)
+            receive(at + k // 2, slabs.at[peers[k]])
+            send(phase, at, k + 1, slabs.at[peers[k]], slabs.at[peers[k]], other)
+        receive(at, slabs.at[pl.ds(0, half)])
 
     for k in order:
-        send(0, k, seq_all.at[me], seq_all.at[me])
+        send(0, AT_X, k, seq_all.at[me], seq_all.at[me])
     loads[3].wait()
     share = cut(me, mine_a)
     for k in far_first:
-        send(5, k, share, share)
-    send(5 + copies, 1, o2_all.at[me], o2_all.at[me])
+        send(4, AT_CUT + k // 2, k, share, share)
+    send(4, AT_CUT, 1, o2_all.at[me], o2_all.at[me])
 
     tokens = n * length
     per_tile = LANES // head_dim
@@ -323,6 +329,8 @@
         slot[me] = dot(x, w[...], 1, 1).astype(BF)
 
     rows_f = [None] * n
+    loads[6].wait()
+    loads[7].wait()
     pick = jnp.where(iota((hi, heads), 0) // length == iota((hi, heads), 1), 1.0, 0.0)
     offs_rep = dot(pick.astype(BF), offs_ref[...]).astype(BF)
     mine = jnp.where(iota((hi, heads), 0) % length == me, pick, 0.0).astype(BF)
@@ -330,24 +338,23 @@
     columns = iota((o_cols, width_d), 1) == iota((o_cols, width_d), 0) + o_cols * me
     columns = jnp.where(columns, 1.0, 0.0).astype(BF)
 
-    for k in order:
-        receive(0, k, seq_all.at[peers[k]])
+    receive(AT_X, seq_all.at[pl.ds(0, n - 1)])
     x = seq_all[:, :, :width_d].astype(F32).reshape(tokens, width_d)
     x_own = dot(x.astype(BF), columns, 1, 1)
     normed = normalize(x).astype(BF)
     loads[0].wait()
     project(normed, w1, pk1)
-    spread(2, pk1)
+    spread(1, AT_PK, pk1)
     for k in near_first:
         share = cut(peers[k], mine_a)
-        receive(5, k, share)
+        receive(AT_CUT + k // 2, share)
         for q in range(1, copies):
-            send(5 + q, k, share, share, me, q)
+            send(4, AT_TWIN + k // 2, k, share, share, me, q)
     con = seq_all[:, :, width_d:].astype(F32).reshape(tokens, channels).astype(BF)
     bias = dot(offs_rep, con, 1, 1)
     own = iota((hi, tokens), 0) % length == iota((hi, tokens), 1) // length
     bias = jnp.where(own, bias, 0.0)
-    collect(2, pk1)
+    collect(1, AT_PK, pk1)
     tied = []
     for t in range(tiles):
         q = split_heads(gathered_tile(pk1, w_cols, t))
@@ -375,16 +382,15 @@
     blended = jnp.concatenate(blended, axis=1)
     loads[1].wait()
     up_all[me, :, :o_cols] = (x_own + dot(blended, o1[...], 1, 1)).astype(BF)
-    spread(3, up_all)
+    spread(2, AT_UP, up_all)
     for k in near_first:
-        for q in range(1, copies):
-            receive(5 + q, k, cut(peers[k], twins[q]))
-        send(5 + copies, k + 1, o2_all.at[peers[k]], o2_all.at[peers[k]], other)
+        receive(AT_TWIN + k // 2, cut(pl.ds(0, copies - 1), 0))
+        send(4, AT_CUT, k + 1, o2_all.at[peers[k]], o2_all.at[peers[k]], other)
 
     add = dot(scores.astype(BF), cw_rep, 0, 0)[:length]
     pair_ref[...] = (seq_all[me, :, width_d:].astype(F32) + add).astype(BF)
 
-    collect(3, up_all)
+    collect(2, AT_UP, up_all)
     updated = jnp.concatenate(
         [up_all[d].astype(F32)[:, :o_cols] for d in range(n)], axis=1
     )
@@ -393,14 +399,13 @@
     loads[2].wait()
     pk2[...] = dot(normed, w2[...], 1, 1).reshape(length, n, w2.shape[0]).astype(BF)
     for k in order:
-        send(4, k, pk2.at[peers[k]], got.at[me])
+        send(3, AT_A2A, k, pk2.at[peers[k]], got.at[me])
     got[me] = pk2[me]
     sel = (iota((n, tokens), 0) == iota((n, tokens), 1) // length) & (
         iota((n, tokens), 1) % length == me
     )
     residual = dot(jnp.where(sel, 1.0, 0.0).astype(BF), updated.astype(BF))
-    for k in order:
-        receive(4, k, got.at[peers[k]])
+    receive(AT_A2A, got.at[pl.ds(0, n - 1)])
     lane_n = iota((n, LANES), 1)
     mixed = []
     for t in range(tiles):
@@ -422,13 +427,24 @@
             total = jnp.where(lane_n >= h * head_dim, both[h * n : (h + 1) * n], total)
         mixed.append(total)
     mixed = jnp.concatenate(mixed, axis=1).astype(BF)
-    land(5 + copies, o2_all)
+    receive(AT_CUT, o2_all.at[pl.ds(0, half)])
     final = jnp.concatenate(
         [dot(mixed, o2_all[d], 1, 1) for d in range(n)], axis=1
     )
     out_ref[...] = (residual + final).astype(BF)
-    for c in sent:
-        c.wait_send()
+    for phase, slabs in enumerate((seq_all, pk1, up_all, got, o2_all)):
+        finish(phase, slabs.at[pl.ds(0, n - 1)])
+
+
+def emit_kernel(out_ref, pair_ref, out_hbm, pair_hbm, sem):
+    copies = [
+        pltpu.make_async_copy(src, dst, sem.at[at])
+        for at, (src, dst) in enumerate(((out_ref, out_hbm), (pair_ref, pair_hbm)))
+    ]
+    for c in copies:
+        c.start()
+    for c in copies:
+        c.wait()
 
 
 def fused_device(n, copies, cuts, seq, spans, con, w1, o1, w2, o2, offs, cw):
@@ -444,11 +460,8 @@
     hbm = pl.BlockSpec(memory_space=pl.ANY)
     out, pair = pl.pallas_call(
         functools.partial(fused_kernel, n, copies, cuts, width // heads),
-        out_shape=(
-            jax.ShapeDtypeStruct((n, width), BF),
-            jax.ShapeDtypeStruct((length, channels), BF),
-        ),
-        in_specs=[hbm, pl.BlockSpec(memory_space=pltpu.SMEM), hbm, vmem, vmem, hbm, hbm, hbm, hbm],
+        out_shape=(pltpu.VMEM((n, width), BF), pltpu.VMEM((length, channels), BF)),
+        in_specs=[hbm, pl.BlockSpec(memory_space=pltpu.SMEM), *[hbm] * 7],
         out_specs=(vmem, vmem),
         scratch_shapes=[
             pltpu.VMEM((window, width), BF),
@@ -460,12 +473,25 @@
             pltpu.VMEM((length, n, window), BF),
             pltpu.VMEM((n, n, window), BF),
             pltpu.VMEM((n, *o2.shape), BF),
-            pltpu.SemaphoreType.DMA((6,)),
-            pltpu.SemaphoreType.DMA((6 + copies, n)),
-            pltpu.SemaphoreType.DMA((6 + copies, n)),
+            pltpu.VMEM(offs.shape, BF),
+            pltpu.VMEM(cw.shape, BF),
+            pltpu.SemaphoreType.DMA((8,)),
+            pltpu.SemaphoreType.DMA((5,)),
+            pltpu.SemaphoreType.DMA((2 + 4 * (n // 2),)),
         ],
         compiler_params=pltpu.CompilerParams(collective_id=0, has_side_effects=True),
     )(seq.reshape(length, width), spans, con.reshape(length, channels), offs, cw, w1, o1, w2, o2)
+    out, pair = (pltpu.with_memory_space_constraint(a, pltpu.VMEM) for a in (out, pair))
+    out, pair = pl.pallas_call(
+        emit_kernel,
+        out_shape=(
+            jax.ShapeDtypeStruct((n, width), BF),
+            jax.ShapeDtypeStruct((length, channels), BF),
+        ),
+        in_specs=[vmem, vmem],
+        out_specs=(hbm, hbm),
+        scratch_shapes=[pltpu.SemaphoreType.DMA((2,))],
+    )(out, pair)
     return out.reshape(n, 1, width), pair.reshape(1, length, channels)
 
 

time: 34.8 us -> 31 us (0.89)
  Pallas kernels: 31.3 us -> 29.4 us
  local copies, waits for them, and re-layouts: 1.89 us -> 0 us
    pallas_call x1, Pallas kernels: 31.3 us -> 28.8 us  [fused_device(): pl.pallas_call(functools.partial(fused_kernel, n, copies, cuts, width //...]
    unnamed x4 -> x0, local copies, waits for them, and re-layouts: 1.89 us -> none
    pallas_call x0 -> x1, Pallas kernels: none -> 0.62 us  [fused_device(): pl.pallas_call(emit_kernel, out_shape=(jax.ShapeDtypeStruct((n, width), B...]
where the time goes in v1:
time: 31 us; the launch traced here: 30.7 us
  Pallas kernels  29.4 us (95%)
  between operations  1.29 us (4%)
    pallas_call x1, Pallas kernels, fused_device(): pl.pallas_call(functools.partial(fused_kernel, n, copies, cuts, width //...  28.8 us
    pallas_call x1, Pallas kernels, fused_device(): pl.pallas_call(emit_kernel, out_shape=(jax.ShapeDtypeStruct((n, width), B...  0.62 us

profile of v1, /device:TPU:0, one launch (start us, length us, event | category | flops | bytes accessed | tf_op | source)
XLA Modules:
  0.0 30.7 jit_solution(5780970009586698370)
XLA Ops:
  1.3 28.8 %shard_map.104 = (bf16[8,768]{1,0:T(8,128)(2,1)S(1)}, bf16[8,128]{1,0:T(8,128)(2,1)S(1)}) custom-call(bf16[8,768]{1,0:T(8,128)(2,1)} %bitcast.13, s32[1]{0:T(128)S(6)} %copy.11.span_ref, bf16[8,128]{1,0:T(8,128)(2,1)} %bitcast.15, bf16[12,128]{1,0:T(8,128)(2,1)} %bitcast.14, bf16[12,128]{1,0:T(8,128)(2,1)} %cw_hbm.1, bf16[288,768]{1,0:T(8,128)(2,1)} %bitcast.9, ...), custom_call_target="tpu_custom_call" | custom-call | tf_op jit(solution)/shard_map/pallas_call | solution.py:461
  30.1 0.6 %shard_map.105 = (bf16[8,768]{1,0:T(8,128)(2,1)}, bf16[8,128]{1,0:T(8,128)(2,1)}) custom-call(bf16[8,768]{1,0:T(8,128)(2,1)S(1)} %get-tuple-element.6.out_ref, bf16[8,128]{1,0:T(8,128)(2,1)S(1)} %get-tuple-element.7.pair_ref), custom_call_target="tpu_custom_call" | custom-call | tf_op jit(solution)/shard_map/pallas_call | solution.py:485
